TPU v7x, 32 devices: a whole 2x2x4 slice. The times are simulated.
32 devices in a mesh: tm: 8 (over z, x), env: 4 (over y, core).
Axes of the slice: x: 2, y: 2, z: 4, core: 2. Of those that a mesh axis runs over, the one named last changes fastest.
Arguments:
- init_state: float32 [70, 1024], P(None, 'env'), may hold values from -6 to 6
- torque: float32 [32, 35, 1024], P('tm', None, 'env'), may hold values from -192 to 192
- contact: int32 [32, 1024], P('tm', 'env'), may hold values 0 or 1
- mass_inverse: float32 [16, 35, 35], P('tm'), may hold values from -0.014 to 1.5, as said below
- stiffness: float32 [35], replicated, may hold values from 10 to 100
- damping: float32 [35], replicated, may hold values from 0.5 to 5
- gravity: float32 [35], replicated, may hold values from 1 to 10
- contact_stiffness: float32 [35], replicated, may hold values from 20 to 100
- contact_damping: float32 [35], replicated, may hold values from 0.5 to 3
Outputs:
- final_states: float32 [16, 70, 1024], P('tm', None, 'env')
- corrections: float32 [3, 1024], P(None, 'env')
Inputs may be any that keep to these rules, and one draw needn't show every extreme that they name: `mass_inverse`: each matrix is symmetric, and each diagonal entry exceeds the sum of the magnitudes of the other entries of its row.
All inputs are finite; a program needn't handle non-finite values. No bound on the sum of `contact` on one device may be relied on, other than what follows from the above.
Results may differ from a plain program's by a relative error of at most 0.00025.
Values sent between devices are 32-bit elements; how exact they have to be, the bound alone decides.
A program may use at most 64 MiB of HBM per device.

v0:
```python
import jax
import jax.numpy as jnp
from jax import lax
from jax.sharding import PartitionSpec as P

DOF = 35
HS = 2
SUB = 32
ITERS = 3
step_length = 0.05


def exact_dot(left, right):
    return jnp.dot(left, right, precision=lax.Precision.HIGHEST, preferred_element_type=jnp.float32)


def coarse_one(state_now, torque_steps, mean_steps, inverse, params):
    stiffness, damping, gravity, contact_stiffness, contact_damping = params
    joint_pos = state_now[:DOF]
    joint_vel = state_now[DOF:]
    for step_pos in range(HS):
        spring = (stiffness + gravity + mean_steps[step_pos] * contact_stiffness)[:, None]
        friction = (damping + mean_steps[step_pos] * contact_damping)[:, None]
        force = torque_steps[step_pos] - spring * joint_pos - friction * joint_vel
        joint_vel = joint_vel + step_length * exact_dot(inverse, force)
        joint_pos = joint_pos + step_length * joint_vel
    return jnp.concatenate([joint_pos, joint_vel], axis=0)


def fine_one(state_now, torque_steps, contact_steps, inverse, params):
    stiffness, damping, gravity, contact_stiffness, contact_damping = params
    fine_dt = step_length / SUB
    joint_pair = (state_now[:DOF], state_now[DOF:])
    for step_pos in range(HS):
        torque_here = torque_steps[step_pos]
        contact_here = contact_steps[step_pos][None, :]

        def substep(counter, pair_now):
            joint_pos, joint_vel = pair_now
            force = (
                torque_here
                - stiffness[:, None] * joint_pos
                - damping[:, None] * joint_vel
                - gravity[:, None] * jnp.sin(joint_pos)
                - contact_here
                * (contact_stiffness[:, None] * joint_pos + contact_damping[:, None] * joint_vel)
            )
            joint_vel = joint_vel + fine_dt * exact_dot(inverse, force)
            joint_pos = joint_pos + fine_dt * joint_vel
            return (joint_pos, joint_vel)

        joint_pair = lax.fori_loop(0, SUB, substep, joint_pair, unroll=min(8, SUB))
    return jnp.concatenate([joint_pair[0], joint_pair[1]], axis=0)


def body(
    init_state,
    torque,
    contact,
    mass_inverse,
    stiffness,
    damping,
    gravity,
    contact_stiffness,
    contact_damping,
):
    params = (stiffness, damping, gravity, contact_stiffness, contact_damping)
    local_slices = mass_inverse.shape[0]
    env_local = init_state.shape[1]
    state_rows = init_state.shape[0]
    torque_steps = torque.reshape(local_slices, HS, DOF, env_local)
    contact_float = contact.astype(jnp.float32)
    contact_steps = contact_float.reshape(local_slices, HS, env_local)
    totals = lax.psum(jnp.sum(contact_float, axis=1), "env")
    mean_steps = (totals / (env_local * lax.axis_size("env"))).reshape(local_slices, HS)
    eye_state = jnp.eye(state_rows, dtype=jnp.float32)
    zero_shift = jnp.zeros((state_rows, env_local), jnp.float32)
    no_force = jnp.zeros((local_slices, HS, DOF, 1), jnp.float32)
    step_maps = jax.vmap(coarse_one, in_axes=(None, 0, 0, 0, None))(
        eye_state, no_force, mean_steps, mass_inverse, params
    )
    coarse_free = jax.vmap(coarse_one, in_axes=(0, 0, 0, 0, None))(
        jnp.zeros((local_slices, state_rows, env_local), jnp.float32),
        torque_steps,
        mean_steps,
        mass_inverse,
        params,
    )
    device_map = eye_state
    for slot_pos in range(local_slices):
        device_map = exact_dot(step_maps[slot_pos], device_map)
    all_maps = lax.all_gather(device_map[None], "tm", axis=0, tiled=True)
    my_index = lax.axis_index("tm")

    def backward(product, inputs):
        position, this_map = inputs
        active = position < my_index
        emitted = jnp.where(active, product, 0.0)
        following = jnp.where(active, exact_dot(product, this_map), eye_state)
        return (following, emitted)

    positions = jnp.arange(lax.axis_size("tm"), dtype=jnp.int32)
    lead_map, phi_rows = lax.scan(backward, eye_state, (positions, all_maps), reverse=True)
    lead_state = exact_dot(lead_map, init_state)

    def sweep(offsets):
        local_shift = zero_shift
        for slot_pos in range(local_slices):
            local_shift = exact_dot(step_maps[slot_pos], local_shift) + offsets[slot_pos]
        entry = lead_state + jnp.einsum(
            "mij,mje->ie",
            phi_rows,
            lax.all_gather(local_shift[None], "tm", axis=0, tiled=True),
            precision=lax.Precision.HIGHEST,
        )
        start_list = []
        end_list = []
        current = entry
        for slot_pos in range(local_slices):
            start_list.append(current)
            current = exact_dot(step_maps[slot_pos], current) + offsets[slot_pos]
            end_list.append(current)
        return (jnp.stack(start_list), jnp.stack(end_list))

    starts, ends = sweep(coarse_free)
    fine_all = jax.vmap(fine_one, in_axes=(0, 0, 0, 0, None))
    records = []
    for iteration in range(ITERS):
        fine_end = fine_all(starts, torque_steps, contact_steps, mass_inverse, params)
        jumps = fine_end - jnp.einsum(
            "sij,sje->sie", step_maps, starts, precision=lax.Precision.HIGHEST
        )
        new_starts, new_ends = sweep(jumps)
        local_max = jnp.max(jnp.sqrt(jnp.sum((new_ends - ends) ** 2, axis=1)), axis=0)
        records.append(lax.pmax(local_max, "tm"))
        starts, ends = (new_starts, new_ends)
    corrections = jnp.stack(records)
    return (ends, corrections)


def solution(mesh):
    placed = (
        P(None, "env"),
        P("tm", None, "env"),
        P("tm", "env"),
        P("tm", None, None),
        P(),
        P(),
        P(),
        P(),
        P(),
    )
    return jax.shard_map(
        body,
        mesh=mesh,
        in_specs=placed,
        out_specs=(P("tm", None, "env"), P(None, "env")),
        check_vma=False,
    )
```

profile of v0, /device:TPU:0, one launch (start us, length us, event | category | flops | bytes accessed | tf_op | source)
XLA Modules:
  0.0 318.0 jit_solution(16330962543061578949)
XLA Ops:
  0.6 0.8 convert_reduce_fusion
  1.5 8.4 %psum.7 = f32[4]{0:T(128)S(1)} all-reduce(f32[4]{0:T(128)S(1)} %convert_reduce_fusion), channel_id=1, replica_groups=mesh['tm'=8,'env'=4] {'env'}, use_global_device_ids=true, to_apply=%region_1.0 | all-reduce | flops 4 | bytes 32 | tf_op jit(solution)/shard_map/psum | solution.py:74
  10.2 0.6 copy-done.4
  10.8 0.6 copy-done.1
  11.8 0.7 copy-done.6
  13.6 31.3 %all-gather.5 = f32[8,70,70]{2,1,0:T(8,128)S(1)} all-gather(f32[1,70,70]{2,1,0:T(8,128)S(1)} %convolution_bitcast_fusion.5), channel_id=2, replica_groups=mesh['tm'=8,'env'=4] {'tm'}, dimensions={0}, use_global_device_ids=true | all-gather | bytes 176400 | tf_op jit(solution)/shard_map/all_gather | solution.py:92
  44.9 12.7 %while.95 = (s32[]{:T(128)}, f32[70,70]{0,1:T(8,128)S(1)}, f32[8,70,70]{1,2,0:T(8,128)S(1)}, s32[8]{0:T(128)S(1)}, s32[]{:T(128)}, /*index=5*/f32[8,70,70]{2,1,0:T(8,128)S(1)}, s32[]{:T(128)}, s32[]{:T(128)}) while((s32[]{:T(128)}, f32[70,70]{0,1:T(8,128)S(1)}, f32[8,70,70]{1,2,0:T(8,128)S(1)}, s32[8]{0:T(128)S(1)}, s32[]{:T(128)}, ...), condition=%wide.region_3.4_spmd.clone, body=%wide.region_2.3_spmd.clone.sunk | while | flops 4135604 | bytes 206392 | solution.py:103
  59.6 31.5 %all-gather.6 = f32[8,70,256]{2,1,0:T(8,128)S(1)} all-gather(f32[1,70,256]{2,1,0:T(8,128)S(1)} %fusion.1027), channel_id=3, replica_groups=mesh['tm'=8,'env'=4] {'tm'}, dimensions={0}, use_global_device_ids=true | all-gather | bytes 645120 | tf_op jit(solution)/shard_map/all_gather | solution.py:113
  91.1 0.7 fusion.1026
  92.3 0.7 copy-done.8
  93.1 17.1 %while.89 = (s32[]{:T(128)}, f32[2,35,256]{2,1,0:T(8,128)S(1)}, f32[2,35,256]{2,1,0:T(8,128)S(1)}, f32[35]{0:T(128)S(1)}, f32[2,35,256]{2,1,0:T(8,128)S(1)}, /*i...) while((s32[]{:T(128)}, f32[2,35,256]{2,1,0:T(8,128)S(1)}, ...), condition=%wide.region_5.6_spmd, body=%wide.region_4.5_spmd.sunk | while | flops 62504960 | bytes 2680981 | solution.py:52
  110.2 17.2 %while.90 = (s32[]{:T(128)}, f32[2,35,256]{2,1,0:T(8,128)S(1)}, f32[2,35,256]{2,1,0:T(8,128)S(1)}, f32[35]{0:T(128)S(1)}, f32[2,35,256]{2,1,0:T(8,128)S(1)}, /*i...) while((s32[]{:T(128)}, f32[2,35,256]{2,1,0:T(8,128)S(1)}, ...), condition=%wide.region_7.8_spmd, body=%wide.region_6.7_spmd.sunk | while | flops 62504960 | bytes 2680981 | solution.py:52
  127.9 31.5 %all-gather.7 = f32[8,70,256]{2,1,0:T(8,128)S(1)} all-gather(f32[1,70,256]{2,1,0:T(8,128)S(1)} %fusion.1025), channel_id=4, replica_groups=mesh['tm'=8,'env'=4] {'tm'}, dimensions={0}, use_global_device_ids=true | all-gather | bytes 645120 | tf_op jit(solution)/shard_map/all_gather | solution.py:113
  159.4 0.7 fusion.1024
  160.5 17.2 %while.91 = (s32[]{:T(128)}, f32[2,35,256]{2,1,0:T(8,128)S(1)}, f32[2,35,256]{2,1,0:T(8,128)S(1)}, f32[35]{0:T(128)S(1)}, f32[2,35,256]{2,1,0:T(8,128)S(1)}, /*i...) while((s32[]{:T(128)}, f32[2,35,256]{2,1,0:T(8,128)S(1)}, ...), condition=%wide.region_9.10_spmd, body=%wide.region_8.9_spmd.sunk | while | flops 62504960 | bytes 2680981 | solution.py:52
  177.7 17.2 %while.92 = (s32[]{:T(128)}, f32[2,35,256]{2,1,0:T(8,128)S(1)}, f32[2,35,256]{2,1,0:T(8,128)S(1)}, f32[35]{0:T(128)S(1)}, f32[2,35,256]{2,1,0:T(8,128)S(1)}, /*i...) while((s32[]{:T(128)}, f32[2,35,256]{2,1,0:T(8,128)S(1)}, ...), condition=%wide.region_11.12_spmd, body=%wide.region_10.11_spmd.sunk | while | flops 62504960 | bytes 2680981 | solution.py:52
  195.3 31.5 %all-gather.8 = f32[8,70,256]{2,1,0:T(8,128)S(1)} all-gather(f32[1,70,256]{2,1,0:T(8,128)S(1)} %fusion.1023), channel_id=5, replica_groups=mesh['tm'=8,'env'=4] {'tm'}, dimensions={0}, use_global_device_ids=true | all-gather | bytes 645120 | tf_op jit(solution)/shard_map/all_gather | solution.py:113
  226.9 0.7 fusion.1022
  228.0 17.2 %while.93 = (s32[]{:T(128)}, f32[2,35,256]{2,1,0:T(8,128)S(1)}, f32[2,35,256]{2,1,0:T(8,128)S(1)}, f32[35]{0:T(128)S(1)}, f32[2,35,256]{2,1,0:T(8,128)S(1)}, /*i...) while((s32[]{:T(128)}, f32[2,35,256]{2,1,0:T(8,128)S(1)}, ...), condition=%wide.region_13.14_spmd, body=%wide.region_12.13_spmd.sunk | while | flops 62504960 | bytes 2680981 | solution.py:52
  245.1 17.2 %while.94 = (s32[]{:T(128)}, f32[2,35,256]{2,1,0:T(8,128)S(1)}, f32[2,35,256]{2,1,0:T(8,128)S(1)}, f32[35]{0:T(128)S(1)}, f32[2,35,256]{2,1,0:T(8,128)S(1)}, /*i...) while((s32[]{:T(128)}, f32[2,35,256]{2,1,0:T(8,128)S(1)}, ...), condition=%wide.region_15.16_spmd, body=%wide.region_14.15_spmd.sunk | while | flops 62504960 | bytes 2680981 | solution.py:52
  262.8 31.3 %all-gather.9 = f32[8,70,256]{2,1,0:T(8,128)S(1)} all-gather(f32[1,70,256]{2,1,0:T(8,128)S(1)} %fusion.1021), channel_id=6, replica_groups=mesh['tm'=8,'env'=4] {'tm'}, dimensions={0}, use_global_device_ids=true | all-gather | bytes 645120 | tf_op jit(solution)/shard_map/all_gather | solution.py:113
  294.2 0.7 fusion.1020
  295.3 0.7 copy.115
  296.1 21.2 %all-reduce = (f32[1,256]{1,0:T(1,128)S(1)}, f32[1,256]{1,0:T(1,128)S(1)}, f32[1,256]{1,0:T(1,128)S(1)}) all-reduce(f32[1,256]{1,0:T(1,128)S(1)} %bitcast.663, f32[1,256]{1,0:T(1,128)S(1)} %bitcast.664, f32[1,256]{1,0:T(1,128)S(1)} %bitcast.662), channel_id=1, replica_groups=mesh['tm'=8,'env'=4] {'tm'}, use_global_device_ids=true, to_apply=%region_24.25 | all-reduce | flops 768 | bytes 6144 | tf_op jit(solution)/shard_map/pmax | solution.py:135
  (294 shorter events, 116.0 us)
Async XLA Ops:
  0.6 56.9 %copy-start = (f32[70,256]{1,0:T(8,128)S(1)}, f32[70,256]{1,0:T(8,128)}, u32[]{:S(2)}) copy-start(f32[70,256]{1,0:T(8,128)} %param.23) | copy-start | bytes 215044
  10.2 0.7 copy-start.4
  10.2 0.7 copy-start.5
  10.8 0.7 copy-start.1
  10.8 0.7 copy-start.2
  10.8 0.7 copy-start.3
  11.8 0.8 copy-start.6
  57.6 0.9 copy-start.7
  92.3 0.7 copy-start.8
where the time goes:
time: 318 us
  blocking collectives  187 us (59%)
  matrix products  111 us (35%)
  local copies, waits for them, and re-layouts  9.75 us (3%)
  loops' own time  7.26 us (2%)
    all_gather x4, blocking collectives, sweep(): lax.all_gather(local_shift[None], 'tm', axis=0, tiled=True)  126 us
    dot_general x220, matrix products, exact_dot(): jnp.dot(left, right, precision=lax.Precision.HIGHEST, preferred_element_t...  108 us
    all_gather x1, blocking collectives, body(): all_maps = lax.all_gather(device_map[None], 'tm', axis=0, tiled=True)  31.3 us
    pmax x1, blocking collectives, body(): records.append(lax.pmax(local_max, 'tm'))  21.2 us
    psum x1, blocking collectives, body(): totals = lax.psum(jnp.sum(contact_float, axis=1), 'env')  8.39 us

commit v1 on v0

--- a/solution.py
+++ b/solution.py
@@ -104,14 +104,40 @@
     lead_state = exact_dot(lead_map, init_state)
 
     def sweep(offsets):
+
+        def link_run_here(inp, row_dim, target):
+            passed = jax.lax.axis_size("tm")
+            v_next, shaped, right_arr = (passed, jax.lax.axis_index("tm"), inp.shape[row_dim])
+            column = []
+            for hop_no in range(v_next):
+                column.append((hop_no, (hop_no + 1) % v_next))
+            heap = []
+            for hop_no in range(v_next):
+                heap.append((hop_no, (hop_no - 1) % v_next))
+            high = v_next // 2
+            formed = later = inp
+            f_now = target(inp, shaped * right_arr)
+            for ix in range(1, high + 1):
+                formed = jax.lax.ppermute(formed, "tm", column)
+                if ix < v_next - high:
+                    later = jax.lax.ppermute(later, "tm", heap)
+                    f_now = f_now + target(later, (shaped + ix) % v_next * right_arr)
+                block_last = target(formed, (shaped - ix) % v_next * right_arr)
+                f_now = f_now + block_last
+            return f_now
+
         local_shift = zero_shift
         for slot_pos in range(local_slices):
             local_shift = exact_dot(step_maps[slot_pos], local_shift) + offsets[slot_pos]
-        entry = lead_state + jnp.einsum(
-            "mij,mje->ie",
-            phi_rows,
-            lax.all_gather(local_shift[None], "tm", axis=0, tiled=True),
-            precision=lax.Precision.HIGHEST,
+        entry = lead_state + link_run_here(
+            local_shift[None],
+            0,
+            lambda own_block, start: jnp.einsum(
+                "mij,mje->ie",
+                lax.dynamic_slice_in_dim(phi_rows, start, own_block.shape[0], axis=0),
+                own_block,
+                precision=lax.Precision.HIGHEST,
+            ),
         )
         start_list = []
         end_list = []

time: 318 us -> 300 us (0.943)
  blocking collectives: 187 us -> 56.5 us
  starting transfers between devices: 0 us -> 58.1 us
  waiting for transfers between devices: 0 us -> 47.4 us
  matrix products: 111 us -> 117 us
    all_gather x4 -> x0, blocking collectives: 126 us -> none  [sweep(): lax.all_gather(local_shift[None], 'tm', axis=0, tiled=True)]
    ppermute x0 -> x28, starting transfers between devices: none -> 58.1 us  [the longest x12 55.6 us: link_run_here(): later = jax.lax.ppermute(later, 'tm', heap)]
    ppermute x0 -> x28, waiting for transfers between devices: none -> 47.4 us  [the longest x16 47.3 us: link_run_here(): formed = jax.lax.ppermute(formed, 'tm', column)]
    dot_general x4 -> x32, matrix products: 2.69 us -> 8.62 us  [sweep(): jnp.einsum('mij,mje->ie', lax.dynamic_slice_in_dim(phi_rows, start, own_b...]
    pmax x1, blocking collectives: 21.2 us -> 17.1 us  [body(): records.append(lax.pmax(local_max, 'tm'))]
  transfers between devices with their start and end apart: 0 -> 28, of which waited for: 0 -> 15; matrix products, arithmetic and copies ran while one was open for 0% -> 5% of each run, Pallas kernels for 0% -> 0%
where the time goes in v1:
time: 300 us; the launch traced here: 299 us
  matrix products  117 us (39%)
  starting transfers between devices  58.1 us (19%)
  blocking collectives  56.5 us (19%)
  waiting for transfers between devices  47.4 us (16%)
  local copies, waits for them, and re-layouts  9.3 us (3%)
  loops' own time  7.21 us (2%)
    dot_general x220, matrix products, exact_dot(): jnp.dot(left, right, precision=lax.Precision.HIGHEST, preferred_element_t...  108 us
    ppermute x12, starting transfers between devices, link_run_here(): later = jax.lax.ppermute(later, 'tm', heap)  55.6 us
    ppermute x16, waiting for transfers between devices, link_run_here(): formed = jax.lax.ppermute(formed, 'tm', column)  47.3 us
    all_gather x1, blocking collectives, body(): all_maps = lax.all_gather(device_map[None], 'tm', axis=0, tiled=True)  31 us
    pmax x1, blocking collectives, body(): records.append(lax.pmax(local_max, 'tm'))  17.1 us
    dot_general x32, matrix products, sweep(): jnp.einsum('mij,mje->ie', lax.dynamic_slice_in_dim(phi_rows, start, own_b...  8.62 us
    psum x1, blocking collectives, body(): totals = lax.psum(jnp.sum(contact_float, axis=1), 'env')  8.4 us
  transfers between devices with their start and end apart: 28, of which 15 were waited for; matrix products, arithmetic and copies ran while one was open for 5% of the time, Pallas kernels for 0%

profile of v1, /device:TPU:0, one launch (start us, length us, event | category | flops | bytes accessed | tf_op | source)
XLA Modules:
  0.0 299.1 jit_solution(4891961708235912567)
XLA Ops:
  1.5 8.4 %psum.7 = f32[4]{0:T(128)S(1)} all-reduce(f32[4]{0:T(128)S(1)} %convert_reduce_fusion), channel_id=1, replica_groups=mesh['tm'=8,'env'=4] {'env'}, use_global_device_ids=true, to_apply=%region_1.0 | all-reduce | flops 4 | bytes 32 | tf_op jit(solution)/shard_map/psum | solution.py:74
  20.1 31.0 %all-gather.1 = f32[8,70,70]{2,1,0:T(8,128)S(1)} all-gather(f32[1,70,70]{2,1,0:T(8,128)S(1)} %convolution_bitcast_fusion.1), channel_id=2, replica_groups=mesh['tm'=8,'env'=4] {'tm'}, dimensions={0}, use_global_device_ids=true | all-gather | bytes 176400 | tf_op jit(solution)/shard_map/all_gather | solution.py:92
  51.1 12.9 %while.95 = (s32[]{:T(128)}, f32[70,70]{0,1:T(8,128)S(1)}, f32[8,70,70]{1,2,0:T(8,128)S(1)}, s32[8]{0:T(128)S(1)}, s32[]{:T(128)}, /*index=5*/f32[8,70,70]{2,1,0:T(8,128)S(1)}, s32[]{:T(128)}, s32[]{:T(128)}) while((s32[]{:T(128)}, f32[70,70]{0,1:T(8,128)S(1)}, f32[8,70,70]{1,2,0:T(8,128)S(1)}, s32[8]{0:T(128)S(1)}, s32[]{:T(128)}, ...), condition=%wide.region_3.4_spmd.clone, body=%wide.region_2.3_spmd.clone.sunk | while | flops 4135604 | bytes 206392 | solution.py:103
  72.3 4.8 %collective-permute-start.4 = (f32[1,70,256]{2,1,0:T(8,128)S(1)}, f32[1,70,256]{2,1,0:T(8,128)S(1)}, u32[]{:S(2)}, u32[]{:S(2)}) collective-permute-start(f32[1,70,256]{2,1,0:T(8,128)S(1)} %collective-permute-done.2), channel_id=1, source_target_pairs={{0,28},{4,0},{8,4},{12,8},{16,12},{20,16},{24,20},{28,24},{1,29},{... | collective-permute-start | bytes 215048 | tf_op jit(solution)/shard_map/ppermute | solution.py:123
  79.6 6.5 %collective-permute-done.6 = f32[1,70,256]{2,1,0:T(8,128)S(1)} collective-permute-done((f32[1,70,256]{2,1,0:T(8,128)S(1)}, f32[1,70,256]{2,1,0:T(8,128)S(1)}, u32[]{:S(2)}, u32[]{:S(2)}) %collective-permute-start.6) | collective-permute-done | bytes 71712 | tf_op jit(solution)/shard_map/ppermute | solution.py:121
  86.6 17.2 %while.89 = (s32[]{:T(128)}, f32[2,35,256]{2,1,0:T(8,128)S(1)}, f32[2,35,256]{2,1,0:T(8,128)S(1)}, f32[35]{0:T(128)S(1)}, f32[2,35,256]{2,1,0:T(8,128)S(1)}, /*i...) while((s32[]{:T(128)}, f32[2,35,256]{2,1,0:T(8,128)S(1)}, ...), condition=%wide.region_5.6_spmd, body=%wide.region_4.5_spmd.sunk | while | flops 62504960 | bytes 2680981 | solution.py:52
  103.8 17.2 %while.90 = (s32[]{:T(128)}, f32[2,35,256]{2,1,0:T(8,128)S(1)}, f32[2,35,256]{2,1,0:T(8,128)S(1)}, f32[35]{0:T(128)S(1)}, f32[2,35,256]{2,1,0:T(8,128)S(1)}, /*i...) while((s32[]{:T(128)}, f32[2,35,256]{2,1,0:T(8,128)S(1)}, ...), condition=%wide.region_7.8_spmd, body=%wide.region_6.7_spmd.sunk | while | flops 62504960 | bytes 2680981 | solution.py:52
  121.8 4.7 %collective-permute-start.7 = (f32[1,70,256]{2,1,0:T(8,128)S(1)}, f32[1,70,256]{2,1,0:T(8,128)S(1)}, u32[]{:S(2)}, u32[]{:S(2)}) collective-permute-start(f32[1,70,256]{2,1,0:T(8,128)S(1)} %bitcast.798), channel_id=1, source_target_pairs={{0,28},{4,0},{8,4},{12,8},{16,12},{20,16},{24,20},{28,24},{1,29},{... | collective-permute-start | bytes 215048 | tf_op jit(solution)/shard_map/ppermute | solution.py:123
  129.3 4.9 %collective-permute-start.9 = (f32[1,70,256]{2,1,0:T(8,128)S(1)}, f32[1,70,256]{2,1,0:T(8,128)S(1)}, u32[]{:S(2)}, u32[]{:S(2)}) collective-permute-start(f32[1,70,256]{2,1,0:T(8,128)S(1)} %collective-permute-done.7), channel_id=1, source_target_pairs={{0,28},{4,0},{8,4},{12,8},{16,12},{20,16},{24,20},{28,24},{1,29},{... | collective-permute-start | bytes 215048 | tf_op jit(solution)/shard_map/ppermute | solution.py:123
  136.7 4.8 %collective-permute-start.11 = (f32[1,70,256]{2,1,0:T(8,128)S(1)}, f32[1,70,256]{2,1,0:T(8,128)S(1)}, u32[]{:S(2)}, u32[]{:S(2)}) collective-permute-start(f32[1,70,256]{2,1,0:T(8,128)S(1)} %collective-permute-done.9), channel_id=1, source_target_pairs={{0,28},{4,0},{8,4},{12,8},{16,12},{20,16},{24,20},{28,24},{1,29},{... | collective-permute-start | bytes 215048 | tf_op jit(solution)/shard_map/ppermute | solution.py:123
  144.4 6.7 %collective-permute-done.13 = f32[1,70,256]{2,1,0:T(8,128)S(1)} collective-permute-done((f32[1,70,256]{2,1,0:T(8,128)S(1)}, f32[1,70,256]{2,1,0:T(8,128)S(1)}, u32[]{:S(2)}, u32[]{:S(2)}) %collective-permute-start.13) | collective-permute-done | bytes 71712 | tf_op jit(solution)/shard_map/ppermute | solution.py:121
  151.6 17.2 %while.91 = (s32[]{:T(128)}, f32[2,35,256]{2,1,0:T(8,128)S(1)}, f32[2,35,256]{2,1,0:T(8,128)S(1)}, f32[35]{0:T(128)S(1)}, f32[2,35,256]{2,1,0:T(8,128)S(1)}, /*i...) while((s32[]{:T(128)}, f32[2,35,256]{2,1,0:T(8,128)S(1)}, ...), condition=%wide.region_9.10_spmd, body=%wide.region_8.9_spmd.sunk | while | flops 62504960 | bytes 2680981 | solution.py:52
  168.8 17.2 %while.92 = (s32[]{:T(128)}, f32[2,35,256]{2,1,0:T(8,128)S(1)}, f32[2,35,256]{2,1,0:T(8,128)S(1)}, f32[35]{0:T(128)S(1)}, f32[2,35,256]{2,1,0:T(8,128)S(1)}, /*i...) while((s32[]{:T(128)}, f32[2,35,256]{2,1,0:T(8,128)S(1)}, ...), condition=%wide.region_11.12_spmd, body=%wide.region_10.11_spmd.sunk | while | flops 62504960 | bytes 2680981 | solution.py:52
  186.8 4.7 %collective-permute-start.14 = (f32[1,70,256]{2,1,0:T(8,128)S(1)}, f32[1,70,256]{2,1,0:T(8,128)S(1)}, u32[]{:S(2)}, u32[]{:S(2)}) collective-permute-start(f32[1,70,256]{2,1,0:T(8,128)S(1)} %bitcast.800), channel_id=1, source_target_pairs={{0,28},{4,0},{8,4},{12,8},{16,12},{20,16},{24,20},{28,24},{1,29},{... | collective-permute-start | bytes 215048 | tf_op jit(solution)/shard_map/ppermute | solution.py:123
  193.8 4.8 %collective-permute-start.16 = (f32[1,70,256]{2,1,0:T(8,128)S(1)}, f32[1,70,256]{2,1,0:T(8,128)S(1)}, u32[]{:S(2)}, u32[]{:S(2)}) collective-permute-start(f32[1,70,256]{2,1,0:T(8,128)S(1)} %collective-permute-done.14), channel_id=1, source_target_pairs={{0,28},{4,0},{8,4},{12,8},{16,12},{20,16},{24,20},{28,24},{1,29},{... | collective-permute-start | bytes 215048 | tf_op jit(solution)/shard_map/ppermute | solution.py:123
  201.2 4.8 %collective-permute-start.18 = (f32[1,70,256]{2,1,0:T(8,128)S(1)}, f32[1,70,256]{2,1,0:T(8,128)S(1)}, u32[]{:S(2)}, u32[]{:S(2)}) collective-permute-start(f32[1,70,256]{2,1,0:T(8,128)S(1)} %collective-permute-done.16), channel_id=1, source_target_pairs={{0,28},{4,0},{8,4},{12,8},{16,12},{20,16},{24,20},{28,24},{1,29},{... | collective-permute-start | bytes 215048 | tf_op jit(solution)/shard_map/ppermute | solution.py:123
  208.8 6.7 %collective-permute-done.20 = f32[1,70,256]{2,1,0:T(8,128)S(1)} collective-permute-done((f32[1,70,256]{2,1,0:T(8,128)S(1)}, f32[1,70,256]{2,1,0:T(8,128)S(1)}, u32[]{:S(2)}, u32[]{:S(2)}) %collective-permute-start.20) | collective-permute-done | bytes 71712 | tf_op jit(solution)/shard_map/ppermute | solution.py:121
  216.1 17.2 %while.93 = (s32[]{:T(128)}, f32[2,35,256]{2,1,0:T(8,128)S(1)}, f32[2,35,256]{2,1,0:T(8,128)S(1)}, f32[35]{0:T(128)S(1)}, f32[2,35,256]{2,1,0:T(8,128)S(1)}, /*i...) while((s32[]{:T(128)}, f32[2,35,256]{2,1,0:T(8,128)S(1)}, ...), condition=%wide.region_13.14_spmd, body=%wide.region_12.13_spmd.sunk | while | flops 62504960 | bytes 2680981 | solution.py:52
  233.3 17.1 %while.94 = (s32[]{:T(128)}, f32[2,35,256]{2,1,0:T(8,128)S(1)}, f32[2,35,256]{2,1,0:T(8,128)S(1)}, f32[35]{0:T(128)S(1)}, f32[2,35,256]{2,1,0:T(8,128)S(1)}, /*i...) while((s32[]{:T(128)}, f32[2,35,256]{2,1,0:T(8,128)S(1)}, ...), condition=%wide.region_15.16_spmd, body=%wide.region_14.15_spmd.sunk | while | flops 62504960 | bytes 2680981 | solution.py:52
  251.3 4.7 %collective-permute-start.21 = (f32[1,70,256]{2,1,0:T(8,128)S(1)}, f32[1,70,256]{2,1,0:T(8,128)S(1)}, u32[]{:S(2)}, u32[]{:S(2)}) collective-permute-start(f32[1,70,256]{2,1,0:T(8,128)S(1)} %bitcast.796), channel_id=1, source_target_pairs={{0,28},{4,0},{8,4},{12,8},{16,12},{20,16},{24,20},{28,24},{1,29},{... | collective-permute-start | bytes 215048 | tf_op jit(solution)/shard_map/ppermute | solution.py:123
  258.3 4.8 %collective-permute-start.23 = (f32[1,70,256]{2,1,0:T(8,128)S(1)}, f32[1,70,256]{2,1,0:T(8,128)S(1)}, u32[]{:S(2)}, u32[]{:S(2)}) collective-permute-start(f32[1,70,256]{2,1,0:T(8,128)S(1)} %collective-permute-done.21), channel_id=1, source_target_pairs={{0,28},{4,0},{8,4},{12,8},{16,12},{20,16},{24,20},{28,24},{1,29},{... | collective-permute-start | bytes 215048 | tf_op jit(solution)/shard_map/ppermute | solution.py:123
  265.7 4.8 %collective-permute-start.25 = (f32[1,70,256]{2,1,0:T(8,128)S(1)}, f32[1,70,256]{2,1,0:T(8,128)S(1)}, u32[]{:S(2)}, u32[]{:S(2)}) collective-permute-start(f32[1,70,256]{2,1,0:T(8,128)S(1)} %collective-permute-done.23), channel_id=1, source_target_pairs={{0,28},{4,0},{8,4},{12,8},{16,12},{20,16},{24,20},{28,24},{1,29},{... | collective-permute-start | bytes 215048 | tf_op jit(solution)/shard_map/ppermute | solution.py:123
  273.1 6.7 %collective-permute-done.27 = f32[1,70,256]{2,1,0:T(8,128)S(1)} collective-permute-done((f32[1,70,256]{2,1,0:T(8,128)S(1)}, f32[1,70,256]{2,1,0:T(8,128)S(1)}, u32[]{:S(2)}, u32[]{:S(2)}) %collective-permute-start.27) | collective-permute-done | bytes 71712 | tf_op jit(solution)/shard_map/ppermute | solution.py:121
  281.4 17.1 %all-reduce = (f32[1,256]{1,0:T(1,128)S(1)}, f32[1,256]{1,0:T(1,128)S(1)}, f32[1,256]{1,0:T(1,128)S(1)}) all-reduce(f32[1,256]{1,0:T(1,128)S(1)} %bitcast.803, f32[1,256]{1,0:T(1,128)S(1)} %bitcast.804, f32[1,256]{1,0:T(1,128)S(1)} %bitcast.802), channel_id=1, replica_groups=mesh['tm'=8,'env'=4] {'tm'}, use_global_device_ids=true, to_apply=%region_24.25 | all-reduce | flops 768 | bytes 6144 | tf_op jit(solution)/shard_map/pmax | solution.py:161
  (374 shorter events, 159.5 us)
Async XLA Ops:
  14.5 50.4 %collective-permute-start.1 = (f32[1,70,256]{2,1,0:T(8,128)S(1)}, f32[1,70,256]{2,1,0:T(8,128)S(1)}, u32[]{:S(2)}, u32[]{:S(2)}) collective-permute-start(f32[1,70,256]{2,1,0:T(8,128)S(1)} %bitcast.793), channel_id=1, source_target_pairs={{0,4},{4,8},{8,12},{12,16},{16,20},{20,24},{24,28},{28,0},{1,5},{5... | collective-permute-start | bytes 215048 | tf_op jit(solution)/shard_map/ppermute | solution.py:121
  16.0 48.9 %collective-permute-start = (f32[1,70,256]{2,1,0:T(8,128)S(1)}, f32[1,70,256]{2,1,0:T(8,128)S(1)}, u32[]{:S(2)}, u32[]{:S(2)}) collective-permute-start(f32[1,70,256]{2,1,0:T(8,128)S(1)} %bitcast.794), channel_id=1, source_target_pairs={{0,28},{4,0},{8,4},{12,8},{16,12},{20,16},{24,20},{28,24},{1,29},{... | collective-permute-start | bytes 215048 | tf_op jit(solution)/shard_map/ppermute | solution.py:123
  64.9 7.1 %collective-permute-start.3 = (f32[1,70,256]{2,1,0:T(8,128)S(1)}, f32[1,70,256]{2,1,0:T(8,128)S(1)}, u32[]{:S(2)}, u32[]{:S(2)}) collective-permute-start(f32[1,70,256]{2,1,0:T(8,128)S(1)} %collective-permute-done.1), channel_id=1, source_target_pairs={{0,4},{4,8},{8,12},{12,16},{16,20},{20,24},{24,28},{28,0},{1,5},{5... | collective-permute-start | bytes 215048 | tf_op jit(solution)/shard_map/ppermute | solution.py:121
  64.9 7.3 %collective-permute-start.2 = (f32[1,70,256]{2,1,0:T(8,128)S(1)}, f32[1,70,256]{2,1,0:T(8,128)S(1)}, u32[]{:S(2)}, u32[]{:S(2)}) collective-permute-start(f32[1,70,256]{2,1,0:T(8,128)S(1)} %collective-permute-done), channel_id=1, source_target_pairs={{0,28},{4,0},{8,4},{12,8},{16,12},{20,16},{24,20},{28,24},{1,29},{... | collective-permute-start | bytes 215048 | tf_op jit(solution)/shard_map/ppermute | solution.py:123
  72.0 7.0 %collective-permute-start.5 = (f32[1,70,256]{2,1,0:T(8,128)S(1)}, f32[1,70,256]{2,1,0:T(8,128)S(1)}, u32[]{:S(2)}, u32[]{:S(2)}) collective-permute-start(f32[1,70,256]{2,1,0:T(8,128)S(1)} %collective-permute-done.3), channel_id=1, source_target_pairs={{0,4},{4,8},{8,12},{12,16},{16,20},{20,24},{24,28},{28,0},{1,5},{5... | collective-permute-start | bytes 215048 | tf_op jit(solution)/shard_map/ppermute | solution.py:121
  79.0 7.1 %collective-permute-start.6 = (f32[1,70,256]{2,1,0:T(8,128)S(1)}, f32[1,70,256]{2,1,0:T(8,128)S(1)}, u32[]{:S(2)}, u32[]{:S(2)}) collective-permute-start(f32[1,70,256]{2,1,0:T(8,128)S(1)} %collective-permute-done.5), channel_id=1, source_target_pairs={{0,4},{4,8},{8,12},{12,16},{16,20},{20,24},{24,28},{28,0},{1,5},{5... | collective-permute-start | bytes 215048 | tf_op jit(solution)/shard_map/ppermute | solution.py:121
  121.7 7.6 %collective-permute-start.8 = (f32[1,70,256]{2,1,0:T(8,128)S(1)}, f32[1,70,256]{2,1,0:T(8,128)S(1)}, u32[]{:S(2)}, u32[]{:S(2)}) collective-permute-start(f32[1,70,256]{2,1,0:T(8,128)S(1)} %bitcast.797), channel_id=1, source_target_pairs={{0,4},{4,8},{8,12},{12,16},{16,20},{20,24},{24,28},{28,0},{1,5},{5... | collective-permute-start | bytes 215048 | tf_op jit(solution)/shard_map/ppermute | solution.py:121
  121.8 7.5 %collective-permute-start.7 = (f32[1,70,256]{2,1,0:T(8,128)S(1)}, f32[1,70,256]{2,1,0:T(8,128)S(1)}, u32[]{:S(2)}, u32[]{:S(2)}) collective-permute-start(f32[1,70,256]{2,1,0:T(8,128)S(1)} %bitcast.798), channel_id=1, source_target_pairs={{0,28},{4,0},{8,4},{12,8},{16,12},{20,16},{24,20},{28,24},{1,29},{... | collective-permute-start | bytes 215048 | tf_op jit(solution)/shard_map/ppermute | solution.py:123
  129.3 7.2 %collective-permute-start.10 = (f32[1,70,256]{2,1,0:T(8,128)S(1)}, f32[1,70,256]{2,1,0:T(8,128)S(1)}, u32[]{:S(2)}, u32[]{:S(2)}) collective-permute-start(f32[1,70,256]{2,1,0:T(8,128)S(1)} %collective-permute-done.8), channel_id=1, source_target_pairs={{0,4},{4,8},{8,12},{12,16},{16,20},{20,24},{24,28},{28,0},{1,5},{5... | collective-permute-start | bytes 215048 | tf_op jit(solution)/shard_map/ppermute | solution.py:121
  129.3 7.5 %collective-permute-start.9 = (f32[1,70,256]{2,1,0:T(8,128)S(1)}, f32[1,70,256]{2,1,0:T(8,128)S(1)}, u32[]{:S(2)}, u32[]{:S(2)}) collective-permute-start(f32[1,70,256]{2,1,0:T(8,128)S(1)} %collective-permute-done.7), channel_id=1, source_target_pairs={{0,28},{4,0},{8,4},{12,8},{16,12},{20,16},{24,20},{28,24},{1,29},{... | collective-permute-start | bytes 215048 | tf_op jit(solution)/shard_map/ppermute | solution.py:123
  136.5 7.0 %collective-permute-start.12 = (f32[1,70,256]{2,1,0:T(8,128)S(1)}, f32[1,70,256]{2,1,0:T(8,128)S(1)}, u32[]{:S(2)}, u32[]{:S(2)}) collective-permute-start(f32[1,70,256]{2,1,0:T(8,128)S(1)} %collective-permute-done.10), channel_id=1, source_target_pairs={{0,4},{4,8},{8,12},{12,16},{16,20},{20,24},{24,28},{28,0},{1,5},{5... | collective-permute-start | bytes 215048 | tf_op jit(solution)/shard_map/ppermute | solution.py:121
  136.7 7.3 %collective-permute-start.11 = (f32[1,70,256]{2,1,0:T(8,128)S(1)}, f32[1,70,256]{2,1,0:T(8,128)S(1)}, u32[]{:S(2)}, u32[]{:S(2)}) collective-permute-start(f32[1,70,256]{2,1,0:T(8,128)S(1)} %collective-permute-done.9), channel_id=1, source_target_pairs={{0,28},{4,0},{8,4},{12,8},{16,12},{20,16},{24,20},{28,24},{1,29},{... | collective-permute-start | bytes 215048 | tf_op jit(solution)/shard_map/ppermute | solution.py:123
  143.8 7.3 %collective-permute-start.13 = (f32[1,70,256]{2,1,0:T(8,128)S(1)}, f32[1,70,256]{2,1,0:T(8,128)S(1)}, u32[]{:S(2)}, u32[]{:S(2)}) collective-permute-start(f32[1,70,256]{2,1,0:T(8,128)S(1)} %collective-permute-done.12), channel_id=1, source_target_pairs={{0,4},{4,8},{8,12},{12,16},{16,20},{20,24},{24,28},{28,0},{1,5},{5... | collective-permute-start | bytes 215048 | tf_op jit(solution)/shard_map/ppermute | solution.py:121
  186.7 7.1 %collective-permute-start.15 = (f32[1,70,256]{2,1,0:T(8,128)S(1)}, f32[1,70,256]{2,1,0:T(8,128)S(1)}, u32[]{:S(2)}, u32[]{:S(2)}) collective-permute-start(f32[1,70,256]{2,1,0:T(8,128)S(1)} %bitcast.799), channel_id=1, source_target_pairs={{0,4},{4,8},{8,12},{12,16},{16,20},{20,24},{24,28},{28,0},{1,5},{5... | collective-permute-start | bytes 215048 | tf_op jit(solution)/shard_map/ppermute | solution.py:121
  193.8 7.0 %collective-permute-start.17 = (f32[1,70,256]{2,1,0:T(8,128)S(1)}, f32[1,70,256]{2,1,0:T(8,128)S(1)}, u32[]{:S(2)}, u32[]{:S(2)}) collective-permute-start(f32[1,70,256]{2,1,0:T(8,128)S(1)} %collective-permute-done.15), channel_id=1, source_target_pairs={{0,4},{4,8},{8,12},{12,16},{16,20},{20,24},{24,28},{28,0},{1,5},{5... | collective-permute-start | bytes 215048 | tf_op jit(solution)/shard_map/ppermute | solution.py:121
  193.8 7.3 %collective-permute-start.16 = (f32[1,70,256]{2,1,0:T(8,128)S(1)}, f32[1,70,256]{2,1,0:T(8,128)S(1)}, u32[]{:S(2)}, u32[]{:S(2)}) collective-permute-start(f32[1,70,256]{2,1,0:T(8,128)S(1)} %collective-permute-done.14), channel_id=1, source_target_pairs={{0,28},{4,0},{8,4},{12,8},{16,12},{20,16},{24,20},{28,24},{1,29},{... | collective-permute-start | bytes 215048 | tf_op jit(solution)/shard_map/ppermute | solution.py:123
  200.9 7.0 %collective-permute-start.19 = (f32[1,70,256]{2,1,0:T(8,128)S(1)}, f32[1,70,256]{2,1,0:T(8,128)S(1)}, u32[]{:S(2)}, u32[]{:S(2)}) collective-permute-start(f32[1,70,256]{2,1,0:T(8,128)S(1)} %collective-permute-done.17), channel_id=1, source_target_pairs={{0,4},{4,8},{8,12},{12,16},{16,20},{20,24},{24,28},{28,0},{1,5},{5... | collective-permute-start | bytes 215048 | tf_op jit(solution)/shard_map/ppermute | solution.py:121
  201.2 7.4 %collective-permute-start.18 = (f32[1,70,256]{2,1,0:T(8,128)S(1)}, f32[1,70,256]{2,1,0:T(8,128)S(1)}, u32[]{:S(2)}, u32[]{:S(2)}) collective-permute-start(f32[1,70,256]{2,1,0:T(8,128)S(1)} %collective-permute-done.16), channel_id=1, source_target_pairs={{0,28},{4,0},{8,4},{12,8},{16,12},{20,16},{24,20},{28,24},{1,29},{... | collective-permute-start | bytes 215048 | tf_op jit(solution)/shard_map/ppermute | solution.py:123
  208.2 7.4 %collective-permute-start.20 = (f32[1,70,256]{2,1,0:T(8,128)S(1)}, f32[1,70,256]{2,1,0:T(8,128)S(1)}, u32[]{:S(2)}, u32[]{:S(2)}) collective-permute-start(f32[1,70,256]{2,1,0:T(8,128)S(1)} %collective-permute-done.19), channel_id=1, source_target_pairs={{0,4},{4,8},{8,12},{12,16},{16,20},{20,24},{24,28},{28,0},{1,5},{5... | collective-permute-start | bytes 215048 | tf_op jit(solution)/shard_map/ppermute | solution.py:121
  251.2 7.1 %collective-permute-start.22 = (f32[1,70,256]{2,1,0:T(8,128)S(1)}, f32[1,70,256]{2,1,0:T(8,128)S(1)}, u32[]{:S(2)}, u32[]{:S(2)}) collective-permute-start(f32[1,70,256]{2,1,0:T(8,128)S(1)} %bitcast.795), channel_id=1, source_target_pairs={{0,4},{4,8},{8,12},{12,16},{16,20},{20,24},{24,28},{28,0},{1,5},{5... | collective-permute-start | bytes 215048 | tf_op jit(solution)/shard_map/ppermute | solution.py:121
  258.3 7.1 %collective-permute-start.24 = (f32[1,70,256]{2,1,0:T(8,128)S(1)}, f32[1,70,256]{2,1,0:T(8,128)S(1)}, u32[]{:S(2)}, u32[]{:S(2)}) collective-permute-start(f32[1,70,256]{2,1,0:T(8,128)S(1)} %collective-permute-done.22), channel_id=1, source_target_pairs={{0,4},{4,8},{8,12},{12,16},{16,20},{20,24},{24,28},{28,0},{1,5},{5... | collective-permute-start | bytes 215048 | tf_op jit(solution)/shard_map/ppermute | solution.py:121
  258.3 7.4 %collective-permute-start.23 = (f32[1,70,256]{2,1,0:T(8,128)S(1)}, f32[1,70,256]{2,1,0:T(8,128)S(1)}, u32[]{:S(2)}, u32[]{:S(2)}) collective-permute-start(f32[1,70,256]{2,1,0:T(8,128)S(1)} %collective-permute-done.21), channel_id=1, source_target_pairs={{0,28},{4,0},{8,4},{12,8},{16,12},{20,16},{24,20},{28,24},{1,29},{... | collective-permute-start | bytes 215048 | tf_op jit(solution)/shard_map/ppermute | solution.py:123
  265.7 7.1 %collective-permute-start.25 = (f32[1,70,256]{2,1,0:T(8,128)S(1)}, f32[1,70,256]{2,1,0:T(8,128)S(1)}, u32[]{:S(2)}, u32[]{:S(2)}) collective-permute-start(f32[1,70,256]{2,1,0:T(8,128)S(1)} %collective-permute-done.23), channel_id=1, source_target_pairs={{0,28},{4,0},{8,4},{12,8},{16,12},{20,16},{24,20},{28,24},{1,29},{... | collective-permute-start | bytes 215048 | tf_op jit(solution)/shard_map/ppermute | solution.py:123
  272.7 7.1 %collective-permute-start.27 = (f32[1,70,256]{2,1,0:T(8,128)S(1)}, f32[1,70,256]{2,1,0:T(8,128)S(1)}, u32[]{:S(2)}, u32[]{:S(2)}) collective-permute-start(f32[1,70,256]{2,1,0:T(8,128)S(1)} %collective-permute-done.26), channel_id=1, source_target_pairs={{0,4},{4,8},{8,12},{12,16},{16,20},{20,24},{24,28},{28,0},{1,5},{5... | collective-permute-start | bytes 215048 | tf_op jit(solution)/shard_map/ppermute | solution.py:121
  (13 other events, 98.0 us)
